TPU v7x, 32 devices: a whole 2x2x4 slice. The times are simulated.
32 devices in a mesh: ctx: 8 (over z, x), tp: 4 (over y, core).
Axes of the slice: x: 2, y: 2, z: 4, core: 2. Of those that a mesh axis runs over, the one named last changes fastest.
Arguments:
- queries: bfloat16 [2048, 8192], P('ctx', 'tp'), may hold values from -8 to 8
- keys: bfloat16 [2048, 1024], P('ctx'), may hold values from -7 to 7
- values: bfloat16 [2048, 1024], P('ctx'), may hold values from -6 to 6
- out_weight: bfloat16 [8192, 4096], P('tp'), may hold values from -0.25 to 0.25
- block_order: int32 [16], P('ctx'), may hold values from 0 to 15, each once
Outputs:
- projected: bfloat16 [2048, 4096], P('ctx', 'tp')
Inputs may be any that keep to these rules, and one draw needn't show every extreme that they name: `block_order`: every sequence block appears exactly once.
All inputs are finite; a program needn't handle non-finite values.
Results may differ from a plain program's by a relative error of at most 0.015.
Values may be sent and summed in bfloat16 or wider, within the bound.
A program may use at most 64 MiB of HBM per device.

v0:
```python
import math
import jax
import jax.numpy as jnp
from jax import lax
from jax.sharding import PartitionSpec as P

QUERY_HEADS = 64
KEY_VALUE_HEADS = 8
HEAD_SIZE = 128


def shards(queries, keys, values, out_weight, block_order):
    tok_rows = queries.shape[0]
    block_len = tok_rows // 2
    heads_dev = queries.shape[1] // HEAD_SIZE
    group_size = QUERY_HEADS // KEY_VALUE_HEADS
    kv_heads = max(1, heads_dev // group_size)
    head_group = heads_dev // kv_heads
    whole_order = lax.all_gather(block_order, "ctx", axis=0, tiled=True)
    offsets = jnp.arange(block_len, dtype=jnp.int32)
    all_pos = (whole_order[:, None] * block_len + offsets[None, :]).reshape(-1)
    local_pos = (block_order[:, None] * block_len + offsets[None, :]).reshape(-1)
    first_head = lax.axis_index("tp") * heads_dev // group_size
    column_start = first_head * HEAD_SIZE
    own_keys = lax.dynamic_slice_in_dim(keys, column_start, kv_heads * HEAD_SIZE, 1)
    own_values = lax.dynamic_slice_in_dim(values, column_start, kv_heads * HEAD_SIZE, 1)
    scale = 1.0 / math.sqrt(HEAD_SIZE)
    query_heads = queries.reshape(tok_rows, kv_heads, head_group, HEAD_SIZE)
    last_pos = jnp.max(local_pos)

    def update(state, key_block, value_block, pos_block):
        run_max, run_sum, accum = state
        keyed = key_block.reshape(-1, kv_heads, HEAD_SIZE)
        valued = value_block.reshape(-1, kv_heads, HEAD_SIZE)
        scores = (
            jnp.einsum("tkgd,skd->kgts", query_heads, keyed, preferred_element_type=jnp.float32)
            * scale
        )
        visible = pos_block[None, None, None, :] <= local_pos[None, None, :, None]
        new_max = jnp.maximum(run_max, jnp.max(jnp.where(visible, scores, -1e30), axis=-1))
        weights = jnp.where(visible, jnp.exp(scores - new_max[..., None]), 0.0)
        factor = jnp.exp(run_max - new_max)
        run_sum = run_sum * factor + jnp.sum(weights, axis=-1)
        spread = jnp.transpose(factor, (2, 0, 1))[..., None]
        accum = accum * spread + jnp.einsum(
            "kgts,skd->tkgd",
            weights.astype(jnp.bfloat16),
            valued,
            preferred_element_type=jnp.float32,
        )
        return (new_max, run_sum, accum)

    start_state = (
        jnp.full((kv_heads, head_group, tok_rows), -1e30, jnp.float32),
        jnp.zeros((kv_heads, head_group, tok_rows), jnp.float32),
        jnp.zeros((tok_rows, kv_heads, head_group, HEAD_SIZE), jnp.float32),
    )
    piece_keys = lax.all_gather(own_keys, "ctx", axis=0, tiled=True)
    piece_values = lax.all_gather(own_values, "ctx", axis=0, tiled=True)
    rows = piece_keys.shape[0]
    step_rows = math.gcd(rows, 512)

    def advance(carry, blocks):
        result = lax.cond(
            jnp.min(blocks[2]) <= last_pos,
            lambda inner: update(inner, blocks[0], blocks[1], blocks[2]),
            lambda inner: inner,
            carry,
        )
        return (result, None)

    stacked = (
        piece_keys.reshape(rows // step_rows, step_rows, -1),
        piece_values.reshape(rows // step_rows, step_rows, -1),
        all_pos.reshape(rows // step_rows, step_rows),
    )
    result, _ = lax.scan(advance, start_state, stacked)
    run_max, run_sum, accum = result
    totals = jnp.transpose(run_sum, (2, 0, 1))[..., None]
    attended = (accum / totals).reshape(tok_rows, heads_dev * HEAD_SIZE).astype(jnp.bfloat16)
    summed = lax.psum_scatter(
        lax.dot_general(
            out_weight, attended, (((0,), (1,)), ((), ())), preferred_element_type=jnp.float32
        ).astype(jnp.bfloat16),
        "tp",
        scatter_dimension=0,
        tiled=True,
    ).astype(jnp.float32)
    return summed.T.astype(jnp.bfloat16)


def solution(mesh):
    in_specs = (P("ctx", "tp"), P("ctx", None), P("ctx", None), P("tp", None), P("ctx"))
    out_specs = P("ctx", "tp")
    return jax.shard_map(shards, mesh=mesh, in_specs=in_specs, out_specs=out_specs, check_vma=False)
```

profile of v0, /device:TPU:0, one launch (start us, length us, event | category | flops | bytes accessed | tf_op | source)
XLA Modules:
  0.0 189.9 jit_solution(12870223693085715618)
XLA Ops:
  6.5 1.0 copy-done
  7.6 0.7 constant_dynamic-slice_fusion.4
  8.3 1.6 constant_dynamic-slice_fusion.3
  10.0 1.3 dynamic-slice
  12.0 0.9 dynamic-update-slice
  12.8 13.1 %all-reduce = s32[16]{0:T(128)S(1)} all-reduce(s32[16]{0:T(128)S(1)} %dynamic-update-slice), channel_id=1, replica_groups=mesh['ctx'=8,'tp'=4] {'ctx'}, use_global_device_ids=true, to_apply=%add | all-reduce | flops 16 | bytes 128
  26.1 1.5 copy.24
  27.5 0.7 copy.26
  28.2 0.7 broadcast_multiply_fusion
  28.9 0.7 add_reduce_fusion
  29.7 22.8 %all-gather.3.cloned.1.call-done = bf16[2048,256]{1,0:T(8,128)(2,1)} async-done(((bf16[256,256]{1,0:T(8,128)(2,1)}), bf16[2048,256]{1,0:T(8,128)(2,1)}) %all-gather.3.cloned.1.call-update) | async-done | bytes 1048592 | tf_op jit(solution)/shard_map/all_gather | solution.py:58
  52.5 1.5 copy.25
  54.0 39.6 %all-gather.5.cloned.1.call-done = bf16[2048,256]{1,0:T(8,128)(2,1)} async-done(((bf16[256,256]{1,0:T(8,128)(2,1)}), bf16[2048,256]{1,0:T(8,128)(2,1)}) %all-gather.5.cloned.1.call-update) | async-done | bytes 1048592 | tf_op jit(solution)/shard_map/all_gather | solution.py:59
  93.7 2.3 %copy.27 = bf16[4,512,256]{1,2,0:T(8,128)(2,1)} copy(bf16[4,512,256]{2,1,0:T(8,128)(2,1)} %bitcast.58) | data formatting | bytes 2097152
  95.9 1.6 broadcast_in_dim.44
  97.5 43.6 %while.15 = (s32[]{:T(128)}, f32[2,8,256]{2,1,0:T(8,128)S(1)}, f32[2,8,256]{2,1,0:T(8,128)S(1)}, f32[256,2,8,128]{3,0,2,1:T(8,128)}, s32[4,512]{1,0:T(4,128)S(1)...) while((s32[]{:T(128)}, f32[2,8,256]{2,1,0:T(8,128)S(1)}, ...), condition=%wide.region_7.8_spmd.clone, body=%wide.region_1.7_spmd.clone.sunk | while | flops 1098003200 | bytes 49555792 | solution.py:77
  97.5 0.6 fusion.23
  99.4 9.0 %conditional.3 = ((f32[2,8,256]{2,1,0:T(8,128)S(1)}, f32[2,8,256]{2,1,0:T(8,128)S(1)}, f32[256,2,8,128]{3,0,2,1:T(8,128)})) conditional(s32[]{:T(128)} %convert_element_type.40, (f32[2,8,256]{2,1,0:T(8,128)S(1)}, f32[2,8,256]{2,1,0:T(8,128)S(1)}, f32[256,2,8,128]{3,0,2,1:T(8,128)}) %tuple.45, (s32[1,512]{1,0:T(1,128)S(1)}, s32[2]{0:T(128)S(1)}, ...), branch_computations={%region_3.3_spmd, %region_4.6_spmd} | conditional | flops 1098002688 | bytes 49550436 | solution.py:64
  99.6 1.0 constant_dynamic-slice_fusion
  100.6 1.5 fusion.2
  102.2 1.7 fusion.6
  103.9 3.2 %bitcast_add_fusion = f32[256,2,8,128]{3,0,2,1:T(8,128)S(1)} fusion(f32[256,2,8,128]{3,0,2,1:T(8,128)S(1)} %copy-done.1, bf16[512,2,128,1]{0,2,3,1:T(8,128)(2,1)S(1)} %bitcast.54, f32[2,512,256,8]{2,1,3,0:T(8,128)S(1)} %get-tuple-element.228, f32[2,8,256]{2,1,0:T(8,128)S(1)} %get-tuple-element.305, pred[256,512]{0,1:T(8,128)(4,1)S(1)} %broadcast_compare_fusion, ...), kind=kOutput, calls=%fused_computation.10 | convolution fusion | flops 546308096 | bytes 13008896 | tf_op jit(solution)/shard_map/while/body/eval_jaxpr/cond/branch_1_fun/kgts,skd->tkgd/dot_general | solution.py:45
  107.1 1.3 copy-done.2
  108.4 0.6 fusion.23
  110.3 9.0 %conditional.3 = ((f32[2,8,256]{2,1,0:T(8,128)S(1)}, f32[2,8,256]{2,1,0:T(8,128)S(1)}, f32[256,2,8,128]{3,0,2,1:T(8,128)})) conditional(s32[]{:T(128)} %convert_element_type.40, (f32[2,8,256]{2,1,0:T(8,128)S(1)}, f32[2,8,256]{2,1,0:T(8,128)S(1)}, f32[256,2,8,128]{3,0,2,1:T(8,128)}) %tuple.45, (s32[1,512]{1,0:T(1,128)S(1)}, s32[2]{0:T(128)S(1)}, ...), branch_computations={%region_3.3_spmd, %region_4.6_spmd} | conditional | flops 1098002688 | bytes 49550436 | solution.py:64
  110.5 1.0 constant_dynamic-slice_fusion
  111.5 1.5 fusion.2
  113.0 1.7 fusion.6
  114.8 3.2 %bitcast_add_fusion = f32[256,2,8,128]{3,0,2,1:T(8,128)S(1)} fusion(f32[256,2,8,128]{3,0,2,1:T(8,128)S(1)} %copy-done.1, bf16[512,2,128,1]{0,2,3,1:T(8,128)(2,1)S(1)} %bitcast.54, f32[2,512,256,8]{2,1,3,0:T(8,128)S(1)} %get-tuple-element.228, f32[2,8,256]{2,1,0:T(8,128)S(1)} %get-tuple-element.305, pred[256,512]{0,1:T(8,128)(4,1)S(1)} %broadcast_compare_fusion, ...), kind=kOutput, calls=%fused_computation.10 | convolution fusion | flops 546308096 | bytes 13008896 | tf_op jit(solution)/shard_map/while/body/eval_jaxpr/cond/branch_1_fun/kgts,skd->tkgd/dot_general | solution.py:45
  117.9 1.3 copy-done.2
  119.3 0.6 fusion.23
  121.1 9.0 %conditional.3 = ((f32[2,8,256]{2,1,0:T(8,128)S(1)}, f32[2,8,256]{2,1,0:T(8,128)S(1)}, f32[256,2,8,128]{3,0,2,1:T(8,128)})) conditional(s32[]{:T(128)} %convert_element_type.40, (f32[2,8,256]{2,1,0:T(8,128)S(1)}, f32[2,8,256]{2,1,0:T(8,128)S(1)}, f32[256,2,8,128]{3,0,2,1:T(8,128)}) %tuple.45, (s32[1,512]{1,0:T(1,128)S(1)}, s32[2]{0:T(128)S(1)}, ...), branch_computations={%region_3.3_spmd, %region_4.6_spmd} | conditional | flops 1098002688 | bytes 49550436 | solution.py:64
  121.4 1.0 constant_dynamic-slice_fusion
  122.4 1.5 fusion.2
  123.9 1.7 fusion.6
  125.7 3.2 %bitcast_add_fusion = f32[256,2,8,128]{3,0,2,1:T(8,128)S(1)} fusion(f32[256,2,8,128]{3,0,2,1:T(8,128)S(1)} %copy-done.1, bf16[512,2,128,1]{0,2,3,1:T(8,128)(2,1)S(1)} %bitcast.54, f32[2,512,256,8]{2,1,3,0:T(8,128)S(1)} %get-tuple-element.228, f32[2,8,256]{2,1,0:T(8,128)S(1)} %get-tuple-element.305, pred[256,512]{0,1:T(8,128)(4,1)S(1)} %broadcast_compare_fusion, ...), kind=kOutput, calls=%fused_computation.10 | convolution fusion | flops 546308096 | bytes 13008896 | tf_op jit(solution)/shard_map/while/body/eval_jaxpr/cond/branch_1_fun/kgts,skd->tkgd/dot_general | solution.py:45
  128.8 1.3 copy-done.2
  130.2 0.6 fusion.23
  132.0 9.0 %conditional.3 = ((f32[2,8,256]{2,1,0:T(8,128)S(1)}, f32[2,8,256]{2,1,0:T(8,128)S(1)}, f32[256,2,8,128]{3,0,2,1:T(8,128)})) conditional(s32[]{:T(128)} %convert_element_type.40, (f32[2,8,256]{2,1,0:T(8,128)S(1)}, f32[2,8,256]{2,1,0:T(8,128)S(1)}, f32[256,2,8,128]{3,0,2,1:T(8,128)}) %tuple.45, (s32[1,512]{1,0:T(1,128)S(1)}, s32[2]{0:T(128)S(1)}, ...), branch_computations={%region_3.3_spmd, %region_4.6_spmd} | conditional | flops 1098002688 | bytes 49550436 | solution.py:64
  132.3 1.0 constant_dynamic-slice_fusion
  133.3 1.5 fusion.2
  134.8 1.7 fusion.6
  136.6 3.2 %bitcast_add_fusion = f32[256,2,8,128]{3,0,2,1:T(8,128)S(1)} fusion(f32[256,2,8,128]{3,0,2,1:T(8,128)S(1)} %copy-done.1, bf16[512,2,128,1]{0,2,3,1:T(8,128)(2,1)S(1)} %bitcast.54, f32[2,512,256,8]{2,1,3,0:T(8,128)S(1)} %get-tuple-element.228, f32[2,8,256]{2,1,0:T(8,128)S(1)} %get-tuple-element.305, pred[256,512]{0,1:T(8,128)(4,1)S(1)} %broadcast_compare_fusion, ...), kind=kOutput, calls=%fused_computation.10 | convolution fusion | flops 546308096 | bytes 13008896 | tf_op jit(solution)/shard_map/while/body/eval_jaxpr/cond/branch_1_fun/kgts,skd->tkgd/dot_general | solution.py:45
  139.7 1.3 copy-done.2
  141.1 1.9 %copy.28 = f32[256,2,8,128]{0,3,2,1:T(8,128)S(1)} copy(f32[256,2,8,128]{3,0,2,1:T(8,128)} %get-tuple-element.142) | data formatting | bytes 4194304 | tf_op jit(solution)/shard_map/while | solution.py:77
  143.0 0.2 divide_convert_fusion
  143.2 11.6 %fusion.15 = bf16[4096,256]{0,1:T(8,128)(2,1)} fusion(bf16[256,2048]{0,1:T(8,128)(2,1)S(1)} %bitcast.55, bf16[2048,4096]{1,0:T(8,128)(2,1)} %param.12), kind=kOutput, calls=%fused_computation.22 | convolution fusion | flops 4296015872 | bytes 19922944 | tf_op jit(solution)/shard_map/dot_general | solution.py:82
  154.8 28.6 %reduce-scatter.2.cloned.1.call-done = bf16[1024,256]{0,1:T(8,128)(2,1)} async-done(((bf16[4096,256]{0,1:T(8,128)(2,1)}), bf16[1024,256]{0,1:T(8,128)(2,1)}) %reduce-scatter.2.cloned.1.call-update) | async-done | bytes 524304 | tf_op jit(solution)/shard_map/reduce_scatter | solution.py:81
  (51 shorter events, 1.3 us)
Async XLA Ops:
  6.5 1.0 copy-start
  6.5 46.0 %all-gather.3.cloned.1.call-start = ((), (), s32[]{:S(2)}) async-start(), calls=%async_computation.1 | async-start | bytes 1179648 | tf_op jit(solution)/shard_map/all_gather | solution.py:58
  8.3 85.4 %all-gather.5.cloned.1.call-start = ((), (), s32[]{:S(2)}) async-start(), calls=%async_computation.2 | async-start | bytes 1179648 | tf_op jit(solution)/shard_map/all_gather | solution.py:59
  9.9 173.5 %reduce-scatter.2.cloned.1.call-start = ((), (), s32[]{:S(2)}) async-start(), calls=%async_computation.3 | async-start | bytes 2621440 | tf_op jit(solution)/shard_map/reduce_scatter | solution.py:81
  100.6 3.3 %copy-start.1 = (f32[256,2,8,128]{3,0,2,1:T(8,128)S(1)}, f32[256,2,8,128]{3,0,2,1:T(8,128)}, u32[]{:S(2)}) copy-start(f32[256,2,8,128]{3,0,2,1:T(8,128)} %get-tuple-element.124) | copy-start | bytes 6291460 | tf_op jit(solution)/shard_map/while/body/eval_jaxpr/cond
  107.0 1.3 copy-start.2
  111.5 3.3 %copy-start.1 = (f32[256,2,8,128]{3,0,2,1:T(8,128)S(1)}, f32[256,2,8,128]{3,0,2,1:T(8,128)}, u32[]{:S(2)}) copy-start(f32[256,2,8,128]{3,0,2,1:T(8,128)} %get-tuple-element.124) | copy-start | bytes 6291460 | tf_op jit(solution)/shard_map/while/body/eval_jaxpr/cond
  117.9 1.3 copy-start.2
  122.4 3.3 %copy-start.1 = (f32[256,2,8,128]{3,0,2,1:T(8,128)S(1)}, f32[256,2,8,128]{3,0,2,1:T(8,128)}, u32[]{:S(2)}) copy-start(f32[256,2,8,128]{3,0,2,1:T(8,128)} %get-tuple-element.124) | copy-start | bytes 6291460 | tf_op jit(solution)/shard_map/while/body/eval_jaxpr/cond
  128.8 1.3 copy-start.2
  133.3 3.3 %copy-start.1 = (f32[256,2,8,128]{3,0,2,1:T(8,128)S(1)}, f32[256,2,8,128]{3,0,2,1:T(8,128)}, u32[]{:S(2)}) copy-start(f32[256,2,8,128]{3,0,2,1:T(8,128)} %get-tuple-element.124) | copy-start | bytes 6291460 | tf_op jit(solution)/shard_map/while/body/eval_jaxpr/cond
  139.7 1.3 copy-start.2
Sparse Core Ops, SparseCore 0:
  9.5 43.0 all-gather.2
  54.6 38.9 all-gather.4
  154.9 28.4 reduce-scatter.1
where the time goes:
time: 190 us
  waiting for transfers between devices  91.2 us (48%)
  matrix products  30.2 us (16%)
  local copies, waits for them, and re-layouts  24.3 us (13%)
  between operations  13.9 us (7%)
  blocking collectives  13.1 us (7%)
  other arithmetic  11.9 us (6%)
  loops' own time  5.26 us (3%)
    all_gather x1, waiting for transfers between devices, shards(): piece_values = lax.all_gather(own_values, 'ctx', axis=0, tiled=True)  39.6 us
    reduce_scatter x1, waiting for transfers between devices, shards(): lax.psum_scatter(lax.dot_general(out_weight, attended, (((0,), (1,)), (()...  28.6 us
    all_gather x1, waiting for transfers between devices, shards(): piece_keys = lax.all_gather(own_keys, 'ctx', axis=0, tiled=True)  22.8 us
    unnamed x1, blocking collectives  13.1 us
    dot_general x4, matrix products, update(): jnp.einsum('kgts,skd->tkgd', weights.astype(jnp.bfloat16), valued, prefer...  12.6 us
    dot_general x1, matrix products, shards(): lax.dot_general(out_weight, attended, (((0,), (1,)), ((), ())), preferred...  11.6 us
    unnamed x10, local copies, waits for them, and re-layouts  9.18 us
    reduce_sum x4, other arithmetic, update(): run_sum = run_sum * factor + jnp.sum(weights, axis=-1)  6.79 us
  transfers between devices with their start and end apart: 3, of which 3 were waited for; matrix products, arithmetic and copies ran while one was open for 5% of the time, Pallas kernels for 0%

commit v1 on v0

--- a/solution.py
+++ b/solution.py
@@ -55,7 +55,12 @@
         jnp.zeros((kv_heads, head_group, tok_rows), jnp.float32),
         jnp.zeros((tok_rows, kv_heads, head_group, HEAD_SIZE), jnp.float32),
     )
-    piece_keys = lax.all_gather(own_keys, "ctx", axis=0, tiled=True)
+    ring = [own_keys]
+    for hop in range(7):
+        ring.append(lax.ppermute(ring[-1], "ctx", [(dev, (dev + 1) % 8) for dev in range(8)]))
+    piece_keys = jnp.roll(
+        jnp.concatenate(ring[::-1], axis=0), (lax.axis_index("ctx") + 1) * ring[0].shape[0], axis=0
+    )
     piece_values = lax.all_gather(own_values, "ctx", axis=0, tiled=True)
     rows = piece_keys.shape[0]
     step_rows = math.gcd(rows, 512)

time: 190 us -> 178 us (0.937)
  waiting for transfers between devices: 91.2 us -> 73.3 us
  starting transfers between devices: 0.09 us -> 5.53 us
    ppermute x0 -> x7, waiting for transfers between devices: none -> 44.8 us  [shards(): lax.ppermute(ring[-1], 'ctx', [(dev, (dev + 1) % 8) for dev in range(8)])]
    all_gather x1, waiting for transfers between devices: 39.6 us -> 0.02 us  [shards(): piece_values = lax.all_gather(own_values, 'ctx', axis=0, tiled=True)]
    all_gather x1 -> x0, waiting for transfers between devices: 22.8 us -> none  [shards(): piece_keys = lax.all_gather(own_keys, 'ctx', axis=0, tiled=True)]
    ppermute x0 -> x7, starting transfers between devices: none -> 5.49 us  [shards(): lax.ppermute(ring[-1], 'ctx', [(dev, (dev + 1) % 8) for dev in range(8)])]
    unnamed x10 -> x25, local copies, waits for them, and re-layouts: 9.18 us -> 9.17 us
  transfers between devices with their start and end apart: 3 -> 9, of which waited for: 3 -> 7; matrix products, arithmetic and copies ran while one was open for 5% -> 6% of each run, Pallas kernels for 0% -> 0%
where the time goes in v1:
time: 178 us
  waiting for transfers between devices  73.3 us (41%)
  matrix products  30.3 us (17%)
  local copies, waits for them, and re-layouts  25.8 us (14%)
  between operations  14.2 us (8%)
  other arithmetic  11.9 us (7%)
  blocking collectives  11.3 us (6%)
  starting transfers between devices  5.53 us (3%)
  loops' own time  5.2 us (3%)
    ppermute x7, waiting for transfers between devices, shards(): lax.ppermute(ring[-1], 'ctx', [(dev, (dev + 1) % 8) for dev in range(8)])  44.8 us
    reduce_scatter x1, waiting for transfers between devices, shards(): lax.psum_scatter(lax.dot_general(out_weight, attended, (((0,), (1,)), (()...  28.5 us
    dot_general x4, matrix products, update(): jnp.einsum('kgts,skd->tkgd', weights.astype(jnp.bfloat16), valued, prefer...  12.6 us
    dot_general x1, matrix products, shards(): lax.dot_general(out_weight, attended, (((0,), (1,)), ((), ())), preferred...  11.6 us
    unnamed x1, blocking collectives  11.3 us
    unnamed x25, local copies, waits for them, and re-layouts  9.17 us
    reduce_sum x4, other arithmetic, update(): run_sum = run_sum * factor + jnp.sum(weights, axis=-1)  6.79 us
    dot_general x4, matrix products, update(): jnp.einsum('tkgd,skd->kgts', query_heads, keyed, preferred_element_type=j...  6.08 us
  transfers between devices with their start and end apart: 9, of which 7 were waited for; matrix products, arithmetic and copies ran while one was open for 6% of the time, Pallas kernels for 0%

profile of v1, /device:TPU:0, one launch (start us, length us, event | category | flops | bytes accessed | tf_op | source)
XLA Modules:
  0.0 177.6 jit_solution(10112030306600190791)
XLA Ops:
  6.5 1.0 constant_dynamic-slice_fusion.5
  7.5 3.0 %collective-permute-start = (bf16[256,256]{1,0:T(8,128)(2,1)S(1)}, bf16[256,256]{1,0:T(8,128)(2,1)S(1)}, u32[]{:S(2)}, u32[]{:S(2)}) collective-permute-start(bf16[256,256]{1,0:T(8,128)(2,1)S(1)} %constant_dynamic-slice_fusion.5), channel_id=1, source_target_pairs={{0,4},{4,8},{8,12},{12,16},{16,20},{20,24},{24,28},{28,0},{1,5},{5... | collective-permute-start | bytes 393224 | tf_op jit(solution)/shard_map/ppermute | solution.py:60
  10.5 6.5 %collective-permute-done = bf16[256,256]{1,0:T(8,128)(2,1)S(1)} collective-permute-done((bf16[256,256]{1,0:T(8,128)(2,1)S(1)}, bf16[256,256]{1,0:T(8,128)(2,1)S(1)}, u32[]{:S(2)}, u32[]{:S(2)}) %collective-permute-start) | collective-permute-done | bytes 131104 | tf_op jit(solution)/shard_map/ppermute | solution.py:60
  17.1 7.7 %collective-permute-done.1 = bf16[256,256]{1,0:T(8,128)(2,1)S(1)} collective-permute-done((bf16[256,256]{1,0:T(8,128)(2,1)S(1)}, bf16[256,256]{1,0:T(8,128)(2,1)S(1)}, u32[]{:S(2)}, u32[]{:S(2)}) %collective-permute-start.1) | collective-permute-done | bytes 131104 | tf_op jit(solution)/shard_map/ppermute | solution.py:60
  24.7 1.2 dynamic-slice
  26.6 0.9 dynamic-update-slice
  28.2 11.3 %all-reduce = s32[16]{0:T(128)S(1)} all-reduce(s32[16]{0:T(128)S(1)} %dynamic-update-slice), channel_id=1, replica_groups=mesh['ctx'=8,'tp'=4] {'ctx'}, use_global_device_ids=true, to_apply=%add | all-reduce | flops 16 | bytes 128
  39.6 2.5 %collective-permute-start.3 = (bf16[256,256]{1,0:T(8,128)(2,1)S(1)}, bf16[256,256]{1,0:T(8,128)(2,1)S(1)}, u32[]{:S(2)}, u32[]{:S(2)}) collective-permute-start(bf16[256,256]{1,0:T(8,128)(2,1)S(1)} %collective-permute-done.2), channel_id=1, source_target_pairs={{0,4},{4,8},{8,12},{12,16},{16,20},{20,24},{24,28},{28,0},{1,5},{5... | collective-permute-start | bytes 393224 | tf_op jit(solution)/shard_map/ppermute | solution.py:60
  42.1 7.7 %collective-permute-done.3 = bf16[256,256]{1,0:T(8,128)(2,1)S(1)} collective-permute-done((bf16[256,256]{1,0:T(8,128)(2,1)S(1)}, bf16[256,256]{1,0:T(8,128)(2,1)S(1)}, u32[]{:S(2)}, u32[]{:S(2)}) %collective-permute-start.3) | collective-permute-done | bytes 131104 | tf_op jit(solution)/shard_map/ppermute | solution.py:60
  49.9 8.7 %collective-permute-done.4 = bf16[256,256]{1,0:T(8,128)(2,1)S(1)} collective-permute-done((bf16[256,256]{1,0:T(8,128)(2,1)S(1)}, bf16[256,256]{1,0:T(8,128)(2,1)S(1)}, u32[]{:S(2)}, u32[]{:S(2)}) %collective-permute-start.4) | collective-permute-done | bytes 131104 | tf_op jit(solution)/shard_map/ppermute | solution.py:60
  58.6 10.0 %collective-permute-done.5 = bf16[256,256]{1,0:T(8,128)(2,1)S(1)} collective-permute-done((bf16[256,256]{1,0:T(8,128)(2,1)S(1)}, bf16[256,256]{1,0:T(8,128)(2,1)S(1)}, u32[]{:S(2)}, u32[]{:S(2)}) %collective-permute-start.5) | collective-permute-done | bytes 131104 | tf_op jit(solution)/shard_map/ppermute | solution.py:60
  69.3 1.5 copy.24
  71.5 0.7 add_reduce_fusion
  72.2 4.1 %collective-permute-done.6 = bf16[256,256]{1,0:T(8,128)(2,1)S(1)} collective-permute-done((bf16[256,256]{1,0:T(8,128)(2,1)S(1)}, bf16[256,256]{1,0:T(8,128)(2,1)S(1)}, u32[]{:S(2)}, u32[]{:S(2)}) %collective-permute-start.6) | collective-permute-done | bytes 131104 | tf_op jit(solution)/shard_map/ppermute | solution.py:60
  76.5 0.9 constant_dynamic-update-slice_fusion.8
  77.5 0.9 constant_dynamic-update-slice_fusion
  78.4 1.1 constant_dynamic-slice_fusion.4
  79.5 1.5 copy.25
  81.1 2.3 %copy.27 = bf16[4,512,256]{1,2,0:T(8,128)(2,1)} copy(bf16[4,512,256]{2,1,0:T(8,128)(2,1)} %bitcast.58) | data formatting | bytes 2097152
  83.4 1.6 broadcast_in_dim.44
  84.9 43.6 %while.15 = (s32[]{:T(128)}, f32[2,8,256]{2,1,0:T(8,128)S(1)}, f32[2,8,256]{2,1,0:T(8,128)S(1)}, f32[256,2,8,128]{3,0,2,1:T(8,128)}, s32[4,512]{1,0:T(4,128)S(1)...) while((s32[]{:T(128)}, f32[2,8,256]{2,1,0:T(8,128)S(1)}, ...), condition=%wide.region_7.8_spmd.clone, body=%wide.region_1.7_spmd.clone.sunk | while | flops 1098003200 | bytes 49555792 | solution.py:82
  86.8 9.0 %conditional.3 = ((f32[2,8,256]{2,1,0:T(8,128)S(1)}, f32[2,8,256]{2,1,0:T(8,128)S(1)}, f32[256,2,8,128]{3,0,2,1:T(8,128)})) conditional(s32[]{:T(128)} %convert_element_type.40, (f32[2,8,256]{2,1,0:T(8,128)S(1)}, f32[2,8,256]{2,1,0:T(8,128)S(1)}, f32[256,2,8,128]{3,0,2,1:T(8,128)}) %tuple.45, (s32[1,512]{1,0:T(1,128)S(1)}, s32[2]{0:T(128)S(1)}, ...), branch_computations={%region_3.3_spmd, %region_4.6_spmd} | conditional | flops 1098002688 | bytes 49550436 | solution.py:69
  87.0 1.0 constant_dynamic-slice_fusion
  88.0 1.5 fusion.2
  89.6 1.7 fusion.6
  91.3 3.2 %bitcast_add_fusion = f32[256,2,8,128]{3,0,2,1:T(8,128)S(1)} fusion(f32[256,2,8,128]{3,0,2,1:T(8,128)S(1)} %copy-done.1, bf16[512,2,128,1]{0,2,3,1:T(8,128)(2,1)S(1)} %bitcast.54, f32[2,512,256,8]{2,1,3,0:T(8,128)S(1)} %get-tuple-element.228, f32[2,8,256]{2,1,0:T(8,128)S(1)} %get-tuple-element.305, pred[256,512]{0,1:T(8,128)(4,1)S(1)} %broadcast_compare_fusion, ...), kind=kOutput, calls=%fused_computation.10 | convolution fusion | flops 546308096 | bytes 13008896 | tf_op jit(solution)/shard_map/while/body/eval_jaxpr/cond/branch_1_fun/kgts,skd->tkgd/dot_general | solution.py:45
  94.5 1.3 copy-done.2
  97.7 9.0 %conditional.3 = ((f32[2,8,256]{2,1,0:T(8,128)S(1)}, f32[2,8,256]{2,1,0:T(8,128)S(1)}, f32[256,2,8,128]{3,0,2,1:T(8,128)})) conditional(s32[]{:T(128)} %convert_element_type.40, (f32[2,8,256]{2,1,0:T(8,128)S(1)}, f32[2,8,256]{2,1,0:T(8,128)S(1)}, f32[256,2,8,128]{3,0,2,1:T(8,128)}) %tuple.45, (s32[1,512]{1,0:T(1,128)S(1)}, s32[2]{0:T(128)S(1)}, ...), branch_computations={%region_3.3_spmd, %region_4.6_spmd} | conditional | flops 1098002688 | bytes 49550436 | solution.py:69
  97.9 1.0 constant_dynamic-slice_fusion
  98.9 1.5 fusion.2
  100.5 1.7 fusion.6
  102.2 3.2 %bitcast_add_fusion = f32[256,2,8,128]{3,0,2,1:T(8,128)S(1)} fusion(f32[256,2,8,128]{3,0,2,1:T(8,128)S(1)} %copy-done.1, bf16[512,2,128,1]{0,2,3,1:T(8,128)(2,1)S(1)} %bitcast.54, f32[2,512,256,8]{2,1,3,0:T(8,128)S(1)} %get-tuple-element.228, f32[2,8,256]{2,1,0:T(8,128)S(1)} %get-tuple-element.305, pred[256,512]{0,1:T(8,128)(4,1)S(1)} %broadcast_compare_fusion, ...), kind=kOutput, calls=%fused_computation.10 | convolution fusion | flops 546308096 | bytes 13008896 | tf_op jit(solution)/shard_map/while/body/eval_jaxpr/cond/branch_1_fun/kgts,skd->tkgd/dot_general | solution.py:45
  105.4 1.3 copy-done.2
  108.6 9.0 %conditional.3 = ((f32[2,8,256]{2,1,0:T(8,128)S(1)}, f32[2,8,256]{2,1,0:T(8,128)S(1)}, f32[256,2,8,128]{3,0,2,1:T(8,128)})) conditional(s32[]{:T(128)} %convert_element_type.40, (f32[2,8,256]{2,1,0:T(8,128)S(1)}, f32[2,8,256]{2,1,0:T(8,128)S(1)}, f32[256,2,8,128]{3,0,2,1:T(8,128)}) %tuple.45, (s32[1,512]{1,0:T(1,128)S(1)}, s32[2]{0:T(128)S(1)}, ...), branch_computations={%region_3.3_spmd, %region_4.6_spmd} | conditional | flops 1098002688 | bytes 49550436 | solution.py:69
  108.8 1.0 constant_dynamic-slice_fusion
  109.8 1.5 fusion.2
  111.4 1.7 fusion.6
  113.1 3.2 %bitcast_add_fusion = f32[256,2,8,128]{3,0,2,1:T(8,128)S(1)} fusion(f32[256,2,8,128]{3,0,2,1:T(8,128)S(1)} %copy-done.1, bf16[512,2,128,1]{0,2,3,1:T(8,128)(2,1)S(1)} %bitcast.54, f32[2,512,256,8]{2,1,3,0:T(8,128)S(1)} %get-tuple-element.228, f32[2,8,256]{2,1,0:T(8,128)S(1)} %get-tuple-element.305, pred[256,512]{0,1:T(8,128)(4,1)S(1)} %broadcast_compare_fusion, ...), kind=kOutput, calls=%fused_computation.10 | convolution fusion | flops 546308096 | bytes 13008896 | tf_op jit(solution)/shard_map/while/body/eval_jaxpr/cond/branch_1_fun/kgts,skd->tkgd/dot_general | solution.py:45
  116.3 1.3 copy-done.2
  119.5 9.0 %conditional.3 = ((f32[2,8,256]{2,1,0:T(8,128)S(1)}, f32[2,8,256]{2,1,0:T(8,128)S(1)}, f32[256,2,8,128]{3,0,2,1:T(8,128)})) conditional(s32[]{:T(128)} %convert_element_type.40, (f32[2,8,256]{2,1,0:T(8,128)S(1)}, f32[2,8,256]{2,1,0:T(8,128)S(1)}, f32[256,2,8,128]{3,0,2,1:T(8,128)}) %tuple.45, (s32[1,512]{1,0:T(1,128)S(1)}, s32[2]{0:T(128)S(1)}, ...), branch_computations={%region_3.3_spmd, %region_4.6_spmd} | conditional | flops 1098002688 | bytes 49550436 | solution.py:69
  119.7 1.0 constant_dynamic-slice_fusion
  120.7 1.5 fusion.2
  122.3 1.7 fusion.6
  124.0 3.2 %bitcast_add_fusion = f32[256,2,8,128]{3,0,2,1:T(8,128)S(1)} fusion(f32[256,2,8,128]{3,0,2,1:T(8,128)S(1)} %copy-done.1, bf16[512,2,128,1]{0,2,3,1:T(8,128)(2,1)S(1)} %bitcast.54, f32[2,512,256,8]{2,1,3,0:T(8,128)S(1)} %get-tuple-element.228, f32[2,8,256]{2,1,0:T(8,128)S(1)} %get-tuple-element.305, pred[256,512]{0,1:T(8,128)(4,1)S(1)} %broadcast_compare_fusion, ...), kind=kOutput, calls=%fused_computation.10 | convolution fusion | flops 546308096 | bytes 13008896 | tf_op jit(solution)/shard_map/while/body/eval_jaxpr/cond/branch_1_fun/kgts,skd->tkgd/dot_general | solution.py:45
  127.2 1.3 copy-done.2
  128.5 1.9 %copy.28 = f32[256,2,8,128]{0,3,2,1:T(8,128)S(1)} copy(f32[256,2,8,128]{3,0,2,1:T(8,128)} %get-tuple-element.142) | data formatting | bytes 4194304 | tf_op jit(solution)/shard_map/while | solution.py:82
  130.7 11.6 %fusion.15 = bf16[4096,256]{0,1:T(8,128)(2,1)} fusion(bf16[256,2048]{0,1:T(8,128)(2,1)S(1)} %bitcast.55, bf16[2048,4096]{1,0:T(8,128)(2,1)} %param.12), kind=kOutput, calls=%fused_computation.22 | convolution fusion | flops 4296015872 | bytes 19922944 | tf_op jit(solution)/shard_map/dot_general | solution.py:87
  142.3 28.5 %reduce-scatter.2.cloned.1.call-done = bf16[1024,256]{0,1:T(8,128)(2,1)} async-done(((bf16[4096,256]{0,1:T(8,128)(2,1)}), bf16[1024,256]{0,1:T(8,128)(2,1)}) %reduce-scatter.2.cloned.1.call-update) | async-done | bytes 524304 | tf_op jit(solution)/shard_map/reduce_scatter | solution.py:86
  (79 shorter events, 6.2 us)
Async XLA Ops:
  6.5 21.0 %copy-start = (bf16[256,1024]{1,0:T(8,128)(2,1)S(1)}, bf16[256,1024]{1,0:T(8,128)(2,1)}, u32[]{:S(2)}) copy-start(bf16[256,1024]{1,0:T(8,128)(2,1)} %param.11) | copy-start | bytes 1572868
  6.5 74.5 %all-gather.2.cloned.1.call-start = ((), (), s32[]{:S(2)}) async-start(), calls=%async_computation.1 | async-start | bytes 1179648 | tf_op jit(solution)/shard_map/all_gather | solution.py:64
  7.5 9.6 %collective-permute-start = (bf16[256,256]{1,0:T(8,128)(2,1)S(1)}, bf16[256,256]{1,0:T(8,128)(2,1)S(1)}, u32[]{:S(2)}, u32[]{:S(2)}) collective-permute-start(bf16[256,256]{1,0:T(8,128)(2,1)S(1)} %constant_dynamic-slice_fusion.5), channel_id=1, source_target_pairs={{0,4},{4,8},{8,12},{12,16},{16,20},{20,24},{24,28},{28,0},{1,5},{5... | collective-permute-start | bytes 393224 | tf_op jit(solution)/shard_map/ppermute | solution.py:60
  17.1 7.7 %collective-permute-start.1 = (bf16[256,256]{1,0:T(8,128)(2,1)S(1)}, bf16[256,256]{1,0:T(8,128)(2,1)S(1)}, u32[]{:S(2)}, u32[]{:S(2)}) collective-permute-start(bf16[256,256]{1,0:T(8,128)(2,1)S(1)} %collective-permute-done), channel_id=1, source_target_pairs={{0,4},{4,8},{8,12},{12,16},{16,20},{20,24},{24,28},{28,0},{1,5},{5... | collective-permute-start | bytes 393224 | tf_op jit(solution)/shard_map/ppermute | solution.py:60
  24.7 14.8 %collective-permute-start.2 = (bf16[256,256]{1,0:T(8,128)(2,1)S(1)}, bf16[256,256]{1,0:T(8,128)(2,1)S(1)}, u32[]{:S(2)}, u32[]{:S(2)}) collective-permute-start(bf16[256,256]{1,0:T(8,128)(2,1)S(1)} %collective-permute-done.1), channel_id=1, source_target_pairs={{0,4},{4,8},{8,12},{12,16},{16,20},{20,24},{24,28},{28,0},{1,5},{5... | collective-permute-start | bytes 393224 | tf_op jit(solution)/shard_map/ppermute | solution.py:60
  28.2 142.5 %reduce-scatter.2.cloned.1.call-start = ((), (), s32[]{:S(2)}) async-start(), calls=%async_computation.2 | async-start | bytes 2621440 | tf_op jit(solution)/shard_map/reduce_scatter | solution.py:86
  39.6 10.3 %collective-permute-start.3 = (bf16[256,256]{1,0:T(8,128)(2,1)S(1)}, bf16[256,256]{1,0:T(8,128)(2,1)S(1)}, u32[]{:S(2)}, u32[]{:S(2)}) collective-permute-start(bf16[256,256]{1,0:T(8,128)(2,1)S(1)} %collective-permute-done.2), channel_id=1, source_target_pairs={{0,4},{4,8},{8,12},{12,16},{16,20},{20,24},{24,28},{28,0},{1,5},{5... | collective-permute-start | bytes 393224 | tf_op jit(solution)/shard_map/ppermute | solution.py:60
  49.8 8.8 %collective-permute-start.4 = (bf16[256,256]{1,0:T(8,128)(2,1)S(1)}, bf16[256,256]{1,0:T(8,128)(2,1)S(1)}, u32[]{:S(2)}, u32[]{:S(2)}) collective-permute-start(bf16[256,256]{1,0:T(8,128)(2,1)S(1)} %collective-permute-done.3), channel_id=1, source_target_pairs={{0,4},{4,8},{8,12},{12,16},{16,20},{20,24},{24,28},{28,0},{1,5},{5... | collective-permute-start | bytes 393224 | tf_op jit(solution)/shard_map/ppermute | solution.py:60
  58.6 10.1 %collective-permute-start.5 = (bf16[256,256]{1,0:T(8,128)(2,1)S(1)}, bf16[256,256]{1,0:T(8,128)(2,1)S(1)}, u32[]{:S(2)}, u32[]{:S(2)}) collective-permute-start(bf16[256,256]{1,0:T(8,128)(2,1)S(1)} %collective-permute-done.4), channel_id=1, source_target_pairs={{0,4},{4,8},{8,12},{12,16},{16,20},{20,24},{24,28},{28,0},{1,5},{5... | collective-permute-start | bytes 393224 | tf_op jit(solution)/shard_map/ppermute | solution.py:60
  68.7 7.7 %collective-permute-start.6 = (bf16[256,256]{1,0:T(8,128)(2,1)S(1)}, bf16[256,256]{1,0:T(8,128)(2,1)S(1)}, u32[]{:S(2)}, u32[]{:S(2)}) collective-permute-start(bf16[256,256]{1,0:T(8,128)(2,1)S(1)} %collective-permute-done.5), channel_id=1, source_target_pairs={{0,4},{4,8},{8,12},{12,16},{16,20},{20,24},{24,28},{28,0},{1,5},{5... | collective-permute-start | bytes 393224 | tf_op jit(solution)/shard_map/ppermute | solution.py:60
  89.6 1.7 copy-start.1
  94.5 1.4 copy-start.2
  100.5 1.7 copy-start.1
  105.4 1.4 copy-start.2
  111.4 1.7 copy-start.1
  116.3 1.4 copy-start.2
  122.3 1.7 copy-start.1
  127.2 1.4 copy-start.2
Sparse Core Ops, SparseCore 0:
  28.3 43.2 all-gather.1
  142.4 28.3 reduce-scatter.1
